TPU v7x, 32 devices: a whole 2x2x4 slice. The times are simulated.
32 devices in a mesh: group: 2 (over y), gx: 4 (over x, core), gy: 4 (over z).
Axes of the slice: x: 2, y: 2, z: 4, core: 2. Of those that a mesh axis runs over, the one named last changes fastest.
Arguments:
- pressure: float32 [192, 64, 768], P(('group', 'gx'), 'gy'), parts along dimension 0, may hold values from -6 to 6
- pressure_prev: float32 [192, 64, 768], P(('group', 'gx'), 'gy'), parts along dimension 0, may hold values from -6 to 6
- courant: float32 [192, 64, 768], P(('group', 'gx'), 'gy'), parts along dimension 0, may hold values from 0.05 to 0.3
- nonlinearity: float32 [192, 64, 768], P(('group', 'gx'), 'gy'), parts along dimension 0, may hold values from 0.03 to 0.3
- absorption: float32 [192, 64, 768], P(('group', 'gx'), 'gy'), parts along dimension 0, may hold values from 0.2 to 2
- own_map: int32 [96, 32], P(('group', 'gx'), 'gy'), parts along dimension 0, may hold values from 0 to 16, as said below
- slot_table: int32 [96, 32], P(('group', 'gx'), 'gy'), parts along dimension 0, may hold values from 0 to 511
- displacement: float32 [128, 128, 384], P(('group', 'gx'), 'gy'), parts along dimension 0, may hold values from -6 to 6
- displacement_prev: float32 [128, 128, 384], P(('group', 'gx'), 'gy'), parts along dimension 0, may hold values from -6 to 6
- layer_labels: int32 [128, 128, 384], P(('group', 'gx'), 'gy'), parts along dimension 0, may hold values from 0 to 3
- shear_table: float32 [8], P('group'), parts along dimension 0, may hold values from 0.05 to 0.15
- viscosity_table: float32 [8], P('group'), parts along dimension 0, may hold values from 0.01 to 0.06
Outputs:
- pressure_mid: float32 [192, 64, 768], P(('group', 'gx'), 'gy'), parts along dimension 0
- pressure_new: float32 [192, 64, 768], P(('group', 'gx'), 'gy'), parts along dimension 0
- tissue_force: float32 [128, 128, 384], P(('group', 'gx'), 'gy'), parts along dimension 0
- displacement_mid: float32 [128, 128, 384], P(('group', 'gx'), 'gy'), parts along dimension 0
- displacement_new: float32 [128, 128, 384], P(('group', 'gx'), 'gy'), parts along dimension 0
There are 2 independent parts, one for each index of `group`. A program takes and returns all parts, laid end to end along the dimension named above; each array names one. Nothing has to cross between parts.
Inputs may be any that keep to these rules, and one draw needn't show every extreme that they name: `own_map`: A value below 16 names tissue block (v // 4, v % 4); 16 marks a line outside the focal zone. Among the lines of one device's block of the map, at most 6 name any one tissue block, and exactly 6 do for some block in every draw.
All inputs are finite; a program needn't handle non-finite values.
Results may differ from a plain program's by a relative error of at most 0.0003.
Values sent between devices are 32-bit elements; how exact they have to be, the bound alone decides.
A program may use at most 64 MiB of HBM per device.

v0:
```python
import jax
import jax.numpy as jnp
from jax import lax
from jax.sharding import PartitionSpec as P


def extended(x, sides, width):
    for axis, dim in sides:
        size, length = (lax.axis_size(axis), x.shape[dim])
        up = [(i, (i + 1) % size) for i in range(size - 1)]
        down = [(j, i) for i, j in up]
        last = lax.slice_in_dim(x, length - width, length, axis=dim)
        first = lax.slice_in_dim(x, 0, width, axis=dim)
        before = lax.ppermute(last, axis, up)
        after = lax.ppermute(first, axis, down)
        x = jnp.concatenate([before, x, after], axis=dim)
    return x


def laplace_ext(ext):
    centre = ext[1:-1, 1:-1]
    zeros = jnp.zeros(centre.shape[:2] + (1,), centre.dtype)
    upper = jnp.concatenate([centre[:, :, 1:], zeros], axis=2)
    lower = jnp.concatenate([zeros, centre[:, :, :-1]], axis=2)
    total = ext[2:, 1:-1] + ext[:-2, 1:-1] + ext[1:-1, 2:] + ext[1:-1, :-2]
    return total + upper + lower - 6.0 * centre


def wave_update(now_ext, before, courant, nonlinearity, absorption):
    now = now_ext[1:-1, 1:-1]
    return (
        2.0 * now
        - before
        + courant * laplace_ext(now_ext)
        + nonlinearity * (now * now - before * before)
        - 0.1 * absorption * (now - before)
    )


def faces_step(now, before, courant, nonlinearity, absorption):
    now_ext = extended(now, (("gx", 0), ("gy", 1)), 1)
    return wave_update(now_ext, before, courant, nonlinearity, absorption)


def layer_lookup(labels, table):
    result = jnp.zeros(labels.shape, jnp.float32)
    for kind in range(table.shape[0]):
        result = result + jnp.where(labels == kind, table[kind], 0.0)
    return result


def elastic_step(now, before, shear, viscosity, force):
    ext = extended(jnp.stack([now, now - before]), (("gx", 1), ("gy", 2)), 1)
    return (
        2.0 * now
        - before
        + shear * laplace_ext(ext[0])
        + viscosity * laplace_ext(ext[1])
        + 0.25 * force
    )


def local(
    pressure,
    pressure_prev,
    courant,
    nonlinearity,
    absorption,
    own_map,
    slot_table,
    displacement,
    displacement_prev,
    layer_labels,
    shear_table,
    viscosity_table,
):
    depth, across, lateral = pressure.shape
    pressure_mid = faces_step(pressure, pressure_prev, courant, nonlinearity, absorption)
    pressure_new = faces_step(pressure_mid, pressure, courant, nonlinearity, absorption)
    force = (
        0.1
        * absorption
        * (pressure_mid * pressure_mid + pressure_new * pressure_new)
        * lax.rsqrt(courant)
    )
    line_count = depth // 2 * (across // 2)
    paired = force.reshape(depth // 2, 2, across // 2, 2, lateral).sum(axis=(1, 3))
    pairing = (
        jnp.arange(lateral, dtype=jnp.int32)[:, None] // 2
        == jnp.arange(lateral // 2, dtype=jnp.int32)[None, :]
    ).astype(jnp.float32)
    lines = (
        jnp.dot(paired.reshape(line_count, lateral), pairing, precision=lax.Precision.HIGHEST)
        * 0.125
    )
    owners = own_map.reshape(line_count)
    places = slot_table.reshape(line_count)
    rows_grid = lax.axis_size("gx")
    cols_grid = lax.axis_size("gy")
    blocks = rows_grid * cols_grid
    capacity = max(2, line_count // blocks)
    order = jnp.arange(line_count, dtype=jnp.int32)
    same_owner = owners[:, None] == owners[None, :]
    rank = jnp.sum(same_owner & (order[None, :] < order[:, None]), axis=1)
    send_index = owners * capacity + rank
    match = jnp.arange(blocks * capacity, dtype=jnp.int32)[:, None] == send_index[None, :]
    send_lines = jnp.dot(match.astype(jnp.float32), lines, precision=lax.Precision.HIGHEST)
    send_places = jnp.sum(jnp.where(match, places[None, :] + 1, 0), axis=1)
    got_lines, got_places = (
        lax.all_to_all(
            send_lines.reshape(blocks, capacity, lateral // 2),
            ("gx", "gy"),
            split_axis=0,
            concat_axis=0,
            tiled=True,
        ),
        lax.all_to_all(
            send_places.reshape(blocks, capacity),
            ("gx", "gy"),
            split_axis=0,
            concat_axis=0,
            tiled=True,
        ),
    )
    tile_rows, tile_cols, tile_depth = displacement.shape
    got_lines = got_lines.reshape(blocks * capacity, tile_depth)
    got_places = got_places.reshape(blocks * capacity)
    landing = jnp.arange(tile_rows * tile_cols, dtype=jnp.int32)[:, None] == got_places[None, :] - 1
    tissue_force = jnp.dot(
        landing.astype(jnp.float32), got_lines, precision=lax.Precision.HIGHEST
    ).reshape(tile_rows, tile_cols, tile_depth)
    shear = layer_lookup(layer_labels, shear_table)
    viscosity = layer_lookup(layer_labels, viscosity_table)
    displacement_mid = elastic_step(displacement, displacement_prev, shear, viscosity, tissue_force)
    displacement_new = elastic_step(displacement_mid, displacement, shear, viscosity, tissue_force)
    return (pressure_mid, pressure_new, tissue_force, displacement_mid, displacement_new)


def solution(mesh):
    return jax.shard_map(
        local,
        mesh=mesh,
        in_specs=(
            P(("group", "gx"), "gy", None),
            P(("group", "gx"), "gy", None),
            P(("group", "gx"), "gy", None),
            P(("group", "gx"), "gy", None),
            P(("group", "gx"), "gy", None),
            P(("group", "gx"), "gy"),
            P(("group", "gx"), "gy"),
            P(("group", "gx"), "gy", None),
            P(("group", "gx"), "gy", None),
            P(("group", "gx"), "gy", None),
            P("group"),
            P("group"),
        ),
        out_specs=(
            P(("group", "gx"), "gy", None),
            P(("group", "gx"), "gy", None),
            P(("group", "gx"), "gy", None),
            P(("group", "gx"), "gy", None),
            P(("group", "gx"), "gy", None),
        ),
        check_vma=False,
    )
```

profile of v0, /device:TPU:0, one launch (start us, length us, event | category | flops | bytes accessed | tf_op | source)
XLA Modules:
  0.0 124.3 jit_solution(6843285488986913172)
XLA Ops:
  0.6 0.7 broadcast_add_fusion
  1.5 0.8 copy.132
  2.7 0.7 all_to_all.9
  3.4 7.4 %all-to-all-start = ((s32[16,1,6]{2,1,0:T(1,128)}), s32[16,1,6]{2,1,0:T(1,128)S(1)}, u32[]{:S(2)}, u32[]{:S(2)}) async-start(s32[16,1,6]{2,1,0:T(1,128)} %bitcast), calls=%async_computation | async-start | bytes 16384 | tf_op jit(solution)/shard_map/all_to_all | solution.py:117
  10.8 0.8 fusion.62
  11.6 1.3 %collective-permute-start = (f32[1,16,768]{2,0,1:T(1,128)S(1)}, f32[1,16,768]{2,0,1:T(1,128)S(1)}, u32[]{:S(2)}, u32[]{:S(2)}) collective-permute-start(f32[1,16,768]{2,0,1:T(1,128)S(1)} %copy.111), channel_id=1, source_target_pairs={{4,0},{8,4},{12,8},{5,1},{9,5},{13,9},{6,2},{10,6},{14,10},{7,3},{... | collective-permute-start | bytes 147464 | tf_op jit(solution)/shard_map/ppermute | solution.py:15
  13.0 3.2 %collective-permute-start.1 = (f32[1,16,768]{2,0,1:T(1,128)S(1)}, f32[1,16,768]{2,0,1:T(1,128)S(1)}, u32[]{:S(2)}, u32[]{:S(2)}) collective-permute-start(f32[1,16,768]{2,0,1:T(1,128)S(1)} %copy.113), channel_id=1, source_target_pairs={{0,4},{4,8},{8,12},{1,5},{5,9},{9,13},{2,6},{6,10},{10,14},{3,7},{... | collective-permute-start | bytes 147464 | tf_op jit(solution)/shard_map/ppermute | solution.py:14
  16.2 1.5 %subtract_bitcast_fusion.1 = f32[1,16,32,384]{3,2,1,0:T(8,128)S(1)} fusion(f32[16,32,384]{2,1,0:T(8,128)} %param.19, f32[16,32,384]{2,1,0:T(8,128)} %param.20), kind=kLoop, calls=%fused_computation.87 | loop fusion | flops 196608 | bytes 2359296 | tf_op jit(solution)/shard_map/stack | solution.py:53
  17.7 3.7 %collective-permute-start.8 = (f32[2,1,32,384]{3,2,1,0:T(8,128)S(1)}, f32[2,1,32,384]{3,2,1,0:T(8,128)S(1)}, u32[]{:S(2)}, u32[]{:S(2)}) collective-permute-start(f32[2,1,32,384]{3,2,1,0:T(8,128)S(1)} %get-tuple-element.43), channel_id=1, source_target_pairs={{0,4},{4,8},{8,12},{1,5},{5,9},{9,13},{2,6},{6,10},{10,14},{3,7},{... | collective-permute-start | bytes 294920 | tf_op jit(solution)/shard_map/ppermute | solution.py:14
  21.4 1.3 %collective-permute-start.9 = (f32[2,1,32,384]{3,2,1,0:T(8,128)S(1)}, f32[2,1,32,384]{3,2,1,0:T(8,128)S(1)}, u32[]{:S(2)}, u32[]{:S(2)}) collective-permute-start(f32[2,1,32,384]{3,2,1,0:T(8,128)S(1)} %get-tuple-element.44), channel_id=1, source_target_pairs={{4,0},{8,4},{12,8},{5,1},{9,5},{13,9},{6,2},{10,6},{14,10},{7,3},{... | collective-permute-start | bytes 294920 | tf_op jit(solution)/shard_map/ppermute | solution.py:15
  22.8 0.7 copy.109
  23.5 0.6 fusion.67
  24.1 0.6 fusion.68
  24.7 1.8 %fusion.61 = (f32[24,16,767]{2,0,1:T(8,128)}, f32[24,16,767]{2,0,1:T(8,128)}) fusion(f32[24,16,768]{2,0,1:T(8,128)S(1)} %copy.109), kind=kLoop, calls=%fused_computation.138 | loop fusion | bytes 4712448 | tf_op jit(solution)/shard_map/slice | solution.py:23
  26.7 1.4 %collective-permute-start.2 = (f32[26,1,768]{2,0,1:T(8,128)S(1)}, f32[26,1,768]{2,0,1:T(8,128)S(1)}, u32[]{:S(2)}, u32[]{:S(2)}) collective-permute-start(f32[26,1,768]{2,0,1:T(8,128)S(1)} %get-tuple-element.47), channel_id=1, source_target_pairs={{1,0},{2,1},{3,2},{5,4},{6,5},{7,6},{9,8},{10,9},{11,10},{13,12},{... | collective-permute-start | bytes 239624 | tf_op jit(solution)/shard_map/ppermute | solution.py:15
  28.1 4.6 %collective-permute-start.3 = (f32[26,1,768]{2,0,1:T(8,128)S(1)}, f32[26,1,768]{2,0,1:T(8,128)S(1)}, u32[]{:S(2)}, u32[]{:S(2)}) collective-permute-start(f32[26,1,768]{2,0,1:T(8,128)S(1)} %get-tuple-element.48), channel_id=1, source_target_pairs={{0,1},{1,2},{2,3},{4,5},{5,6},{6,7},{8,9},{9,10},{10,11},{12,13},{... | collective-permute-start | bytes 239624 | tf_op jit(solution)/shard_map/ppermute | solution.py:14
  32.8 3.5 %collective-permute-start.10 = (f32[2,18,1,384]{3,2,1,0:T(1,128)S(1)}, f32[2,18,1,384]{3,2,1,0:T(1,128)S(1)}, u32[]{:S(2)}, u32[]{:S(2)}) collective-permute-start(f32[2,18,1,384]{3,2,1,0:T(1,128)S(1)} %get-tuple-element.39), channel_id=1, source_target_pairs={{0,1},{1,2},{2,3},{4,5},{5,6},{6,7},{8,9},{9,10},{10,11},{12,13},{... | collective-permute-start | bytes 165896 | tf_op jit(solution)/shard_map/ppermute | solution.py:14
  36.4 1.3 %collective-permute-start.11 = (f32[2,18,1,384]{3,2,1,0:T(1,128)S(1)}, f32[2,18,1,384]{3,2,1,0:T(1,128)S(1)}, u32[]{:S(2)}, u32[]{:S(2)}) collective-permute-start(f32[2,18,1,384]{3,2,1,0:T(1,128)S(1)} %get-tuple-element.40), channel_id=1, source_target_pairs={{1,0},{2,1},{3,2},{5,4},{6,5},{7,6},{9,8},{10,9},{11,10},{13,12},{... | collective-permute-start | bytes 165896 | tf_op jit(solution)/shard_map/ppermute | solution.py:15
  37.7 6.1 %fusion.17 = f32[24,16,768]{2,0,1:T(8,128)S(1)} fusion(f32[26,1,768]{2,0,1:T(8,128)S(1)} %collective-permute-done.3, f32[1,16,768]{2,0,1:T(1,128)S(1)} %collective-permute-done, f32[24,16,768]{2,0,1:T(8,128)S(1)} %copy.109, f32[1,16,768]{2,0,1:T(1,128)S(1)} %collective-permute-done.1, f32[26,1,768]{2,0,1:T(8,128)S(1)} %collective-permute-done.2, ...), kind=kLoop, calls=%fused_computation.28 | loop fusion | flops 8257536 | bytes 9692160 | tf_op jit(solution)/shard_map/sub | solution.py:32
  43.8 0.4 fusion.60
  44.3 2.2 %collective-permute-start.5 = (f32[1,16,768]{2,0,1:T(1,128)S(1)}, f32[1,16,768]{2,0,1:T(1,128)S(1)}, u32[]{:S(2)}, u32[]{:S(2)}) collective-permute-start(f32[1,16,768]{2,0,1:T(1,128)S(1)} %get-tuple-element.49), channel_id=1, source_target_pairs={{0,4},{4,8},{8,12},{1,5},{5,9},{9,13},{2,6},{6,10},{10,14},{3,7},{... | collective-permute-start | bytes 147464 | tf_op jit(solution)/shard_map/ppermute | solution.py:14
  46.5 1.3 %collective-permute-start.4 = (f32[1,16,768]{2,0,1:T(1,128)S(1)}, f32[1,16,768]{2,0,1:T(1,128)S(1)}, u32[]{:S(2)}, u32[]{:S(2)}) collective-permute-start(f32[1,16,768]{2,0,1:T(1,128)S(1)} %get-tuple-element.50), channel_id=1, source_target_pairs={{4,0},{8,4},{12,8},{5,1},{9,5},{13,9},{6,2},{10,6},{14,10},{7,3},{... | collective-permute-start | bytes 147464 | tf_op jit(solution)/shard_map/ppermute | solution.py:15
  48.1 3.3 %collective-permute-done.4 = f32[1,16,768]{2,0,1:T(1,128)S(1)} collective-permute-done((f32[1,16,768]{2,0,1:T(1,128)S(1)}, f32[1,16,768]{2,0,1:T(1,128)S(1)}, u32[]{:S(2)}, u32[]{:S(2)}) %collective-permute-start.4) | collective-permute-done | bytes 49184 | tf_op jit(solution)/shard_map/ppermute | solution.py:15
  51.5 1.3 %collective-permute-start.6 = (f32[26,1,768]{2,0,1:T(8,128)S(1)}, f32[26,1,768]{2,0,1:T(8,128)S(1)}, u32[]{:S(2)}, u32[]{:S(2)}) collective-permute-start(f32[26,1,768]{2,0,1:T(8,128)S(1)} %get-tuple-element.45), channel_id=1, source_target_pairs={{1,0},{2,1},{3,2},{5,4},{6,5},{7,6},{9,8},{10,9},{11,10},{13,12},{... | collective-permute-start | bytes 239624 | tf_op jit(solution)/shard_map/ppermute | solution.py:15
  52.8 5.3 %collective-permute-start.7 = (f32[26,1,768]{2,0,1:T(8,128)S(1)}, f32[26,1,768]{2,0,1:T(8,128)S(1)}, u32[]{:S(2)}, u32[]{:S(2)}) collective-permute-start(f32[26,1,768]{2,0,1:T(8,128)S(1)} %get-tuple-element.46), channel_id=1, source_target_pairs={{0,1},{1,2},{2,3},{4,5},{5,6},{6,7},{8,9},{9,10},{10,11},{12,13},{... | collective-permute-start | bytes 239624 | tf_op jit(solution)/shard_map/ppermute | solution.py:14
  58.3 0.3 collective-permute-done.6
  58.6 1.7 %collective-permute-done.7 = f32[26,1,768]{2,0,1:T(8,128)S(1)} collective-permute-done((f32[26,1,768]{2,0,1:T(8,128)S(1)}, f32[26,1,768]{2,0,1:T(8,128)S(1)}, u32[]{:S(2)}, u32[]{:S(2)}) %collective-permute-start.7) | collective-permute-done | bytes 79904 | tf_op jit(solution)/shard_map/ppermute | solution.py:14
  60.3 5.1 %rsqrt_multiply_fusion = (f32[24,16,768]{2,0,1:T(8,128)}, f32[24,16,768]{2,0,1:T(8,128)}) fusion(f32[24,16,768]{2,0,1:T(8,128)S(1)} %fusion.17, f32[24,16,768]{2,1,0:T(8,128)S(1)} %copy-done.9, f32[24,16,768]{2,1,0:T(8,128)S(1)} %copy-done.10, f32[24,16,768]{2,1,0:T(8,128)S(1)} %copy-done.8, f32[24,16,767]{2,0,1:T(8,128)S(1)} %get-tuple-element.52, ...), kind=kLoop, calls=%fused_computation.40 | loop fusion | flops 9437184 | bytes 10871808 | tf_op jit(solution)/shard_map/mul | solution.py:81
  65.4 2.9 %reshape.115 = f32[12,2,8,2,768]{4,1,0,3,2:T(2,128)} reshape(f32[24,16,768]{2,0,1:T(8,128)} %get-tuple-element.31) | data formatting | bytes 2359296 | tf_op jit(solution)/shard_map/reshape | solution.py:87
  68.3 2.9 %reduce_sum.29 = f32[12,8,768]{2,0,1:T(8,128)} reduce(f32[12,2,8,2,768]{4,1,0,3,2:T(2,128)} %reshape.115, f32[]{:T(128)} %constant.14.clone.1), dimensions={1,3}, to_apply=%region_2.3 | reduce | flops 221184 | bytes 1474564 | tf_op jit(solution)/shard_map/reduce_sum | solution.py:87
  71.2 1.7 %fusion.21 = f32[96,384]{1,0:T(8,128)S(1)} fusion(s32[768]{0:T(1024)S(1)} %add_select_fusion, f32[12,8,768]{2,0,1:T(8,128)} %reduce_sum.29), kind=kOutput, calls=%fused_computation.42 | convolution fusion | flops 340070400 | bytes 445440 | tf_op jit(solution)/shard_map/dot_general | solution.py:93
  73.1 0.7 reshape.117
  73.8 8.3 %all-to-all-start.1 = ((f32[16,6,384]{2,1,0:T(8,128)}), f32[16,6,384]{2,1,0:T(8,128)}, u32[]{:S(2)}, u32[]{:S(2)}) async-start(f32[16,6,384]{2,1,0:T(8,128)} %reshape.117), calls=%async_computation.1 | async-start | bytes 393216 | tf_op jit(solution)/shard_map/all_to_all | solution.py:110
  82.1 2.3 %fusion.65 = (f32[16,32,383]{2,1,0:T(8,128)}, f32[16,32,383]{2,1,0:T(8,128)}, f32[16,32,383]{2,1,0:T(8,128)}, f32[16,32,383]{2,1,0:T(8,128)}) fusion(f32[18,34,384]{2,1,0:T(8,128)S(1)} %get-tuple-element.35, f32[18,34,384]{2,1,0:T(8,128)S(1)} %get-tuple-element.36), kind=kLoop, calls=%fused_computation.142 | loop fusion | bytes 6275072 | tf_op jit(solution)/shard_map/slice | solution.py:23
  84.4 5.8 %all-to-all-done.1 = f32[16,6,384]{2,1,0:T(8,128)} async-done(((f32[16,6,384]{2,1,0:T(8,128)}), f32[16,6,384]{2,1,0:T(8,128)}, u32[]{:S(2)}, u32[]{:S(2)}) %all-to-all-start.1) | async-done | bytes 147488 | tf_op jit(solution)/shard_map/all_to_all | solution.py:110
  90.2 0.9 reshape.119
  91.2 0.5 fusion.47
  91.7 0.6 copy-done.1
  92.3 8.6 %subtract_bitcast_fusion = (f32[1,16,32,384]{3,2,1,0:T(8,128)S(1)}, f32[16,32,384]{2,1,0:T(8,128)S(1)}, pred[16,32,384]{2,1,0:T(8,128)(4,1)S(1)}, pred[16,32,384...) fusion(f32[16,32,384]{2,1,0:T(8,128)S(1)} %copy-done.1, ...), kind=kLoop, calls=%fused_computation.85 | loop fusion | flops 8060928 | bytes 16506912 | tf_op jit(solution)/shard_map/stack | solution.py:53
  100.9 2.2 %collective-permute-start.12 = (f32[2,1,32,384]{3,2,1,0:T(8,128)S(1)}, f32[2,1,32,384]{3,2,1,0:T(8,128)S(1)}, u32[]{:S(2)}, u32[]{:S(2)}) collective-permute-start(f32[2,1,32,384]{3,2,1,0:T(8,128)S(1)} %get-tuple-element.41), channel_id=1, source_target_pairs={{0,4},{4,8},{8,12},{1,5},{5,9},{9,13},{2,6},{6,10},{10,14},{3,7},{... | collective-permute-start | bytes 294920 | tf_op jit(solution)/shard_map/ppermute | solution.py:14
  103.1 1.3 %collective-permute-start.13 = (f32[2,1,32,384]{3,2,1,0:T(8,128)S(1)}, f32[2,1,32,384]{3,2,1,0:T(8,128)S(1)}, u32[]{:S(2)}, u32[]{:S(2)}) collective-permute-start(f32[2,1,32,384]{3,2,1,0:T(8,128)S(1)} %get-tuple-element.42), channel_id=1, source_target_pairs={{4,0},{8,4},{12,8},{5,1},{9,5},{13,9},{6,2},{10,6},{14,10},{7,3},{... | collective-permute-start | bytes 294920 | tf_op jit(solution)/shard_map/ppermute | solution.py:15
  104.4 2.5 %collective-permute-done.13 = f32[2,1,32,384]{3,2,1,0:T(8,128)S(1)} collective-permute-done((f32[2,1,32,384]{3,2,1,0:T(8,128)S(1)}, f32[2,1,32,384]{3,2,1,0:T(8,128)S(1)}, u32[]{:S(2)}, u32[]{:S(2)}) %collective-permute-start.13) | collective-permute-done | bytes 98336 | tf_op jit(solution)/shard_map/ppermute | solution.py:15
  107.0 2.8 %collective-permute-start.14 = (f32[2,18,1,384]{3,2,1,0:T(1,128)S(1)}, f32[2,18,1,384]{3,2,1,0:T(1,128)S(1)}, u32[]{:S(2)}, u32[]{:S(2)}) collective-permute-start(f32[2,18,1,384]{3,2,1,0:T(1,128)S(1)} %get-tuple-element.37), channel_id=1, source_target_pairs={{0,1},{1,2},{2,3},{4,5},{5,6},{6,7},{8,9},{9,10},{10,11},{12,13},{... | collective-permute-start | bytes 165896 | tf_op jit(solution)/shard_map/ppermute | solution.py:14
  109.8 1.4 %collective-permute-start.15 = (f32[2,18,1,384]{3,2,1,0:T(1,128)S(1)}, f32[2,18,1,384]{3,2,1,0:T(1,128)S(1)}, u32[]{:S(2)}, u32[]{:S(2)}) collective-permute-start(f32[2,18,1,384]{3,2,1,0:T(1,128)S(1)} %get-tuple-element.38), channel_id=1, source_target_pairs={{1,0},{2,1},{3,2},{5,4},{6,5},{7,6},{9,8},{10,9},{11,10},{13,12},{... | collective-permute-start | bytes 165896 | tf_op jit(solution)/shard_map/ppermute | solution.py:15
  111.2 1.4 %copy.137 = f32[24,16,768]{2,1,0:T(8,128)} copy(f32[24,16,768]{2,0,1:T(8,128)S(1)} %fusion.17) | data formatting | bytes 2359296
  112.6 1.4 %copy.138 = f32[24,16,768]{2,1,0:T(8,128)} copy(f32[24,16,768]{2,0,1:T(8,128)S(1)} %copy-done.11) | data formatting | bytes 2359296
  113.9 2.0 %collective-permute-done.15 = f32[2,18,1,384]{3,2,1,0:T(1,128)S(1)} collective-permute-done((f32[2,18,1,384]{3,2,1,0:T(1,128)S(1)}, f32[2,18,1,384]{3,2,1,0:T(1,128)S(1)}, u32[]{:S(2)}, u32[]{:S(2)}) %collective-permute-start.15) | collective-permute-done | bytes 55328 | tf_op jit(solution)/shard_map/ppermute | solution.py:15
  117.0 7.3 %fusion.25 = f32[16,32,384]{2,1,0:T(8,128)} fusion(f32[18,34,384]{2,1,0:T(8,128)S(1)} %get-tuple-element.34, f32[18,34,384]{2,1,0:T(8,128)S(1)} %get-tuple-element.33, f32[16,32,383]{2,1,0:T(8,128)S(1)} %get-tuple-element.60, f32[16,32,383]{2,1,0:T(8,128)S(1)} %get-tuple-element.59, f32[16,32,383]{2,1,0:T(8,128)S(1)} %get-tuple-element.58, ...), kind=kLoop, calls=%fused_computation.51 | loop fusion | flops 7077888 | bytes 14934048 | tf_op jit(solution)/shard_map/add | solution.py:55
  (65 shorter events, 2.9 us)
Async XLA Ops:
  3.4 23.1 %all-to-all-start = ((s32[16,1,6]{2,1,0:T(1,128)}), s32[16,1,6]{2,1,0:T(1,128)S(1)}, u32[]{:S(2)}, u32[]{:S(2)}) async-start(s32[16,1,6]{2,1,0:T(1,128)} %bitcast), calls=%async_computation | async-start | bytes 16384 | tf_op jit(solution)/shard_map/all_to_all | solution.py:117
  11.6 15.0 %collective-permute-start = (f32[1,16,768]{2,0,1:T(1,128)S(1)}, f32[1,16,768]{2,0,1:T(1,128)S(1)}, u32[]{:S(2)}, u32[]{:S(2)}) collective-permute-start(f32[1,16,768]{2,0,1:T(1,128)S(1)} %copy.111), channel_id=1, source_target_pairs={{4,0},{8,4},{12,8},{5,1},{9,5},{13,9},{6,2},{10,6},{14,10},{7,3},{... | collective-permute-start | bytes 147464 | tf_op jit(solution)/shard_map/ppermute | solution.py:15
  13.0 4.7 %copy-start = (f32[16,32,384]{2,1,0:T(8,128)S(1)}, f32[16,32,384]{2,1,0:T(8,128)}, u32[]{:S(2)}) copy-start(f32[16,32,384]{2,1,0:T(8,128)} %param.19) | copy-start | bytes 2359300
  13.0 13.6 %collective-permute-start.1 = (f32[1,16,768]{2,0,1:T(1,128)S(1)}, f32[1,16,768]{2,0,1:T(1,128)S(1)}, u32[]{:S(2)}, u32[]{:S(2)}) collective-permute-start(f32[1,16,768]{2,0,1:T(1,128)S(1)} %copy.113), channel_id=1, source_target_pairs={{0,4},{4,8},{8,12},{1,5},{5,9},{9,13},{2,6},{6,10},{10,14},{3,7},{... | collective-permute-start | bytes 147464 | tf_op jit(solution)/shard_map/ppermute | solution.py:14
  17.7 15.1 %copy-start.3 = (f32[1,16,32,384]{3,2,1,0:T(8,128)}, f32[1,16,32,384]{3,2,1,0:T(8,128)S(1)}, u32[]{:S(2)}) copy-start(f32[1,16,32,384]{3,2,1,0:T(8,128)S(1)} %subtract_bitcast_fusion.1) | copy-start | bytes 2359300
  17.7 5.1 %copy-start.6 = (f32[24,16,768]{2,1,0:T(8,128)S(1)}, f32[24,16,768]{2,1,0:T(8,128)}, u32[]{:S(2)}) copy-start(f32[24,16,768]{2,1,0:T(8,128)} %param.12) | copy-start | bytes 3538948
  17.7 15.0 %collective-permute-start.8 = (f32[2,1,32,384]{3,2,1,0:T(8,128)S(1)}, f32[2,1,32,384]{3,2,1,0:T(8,128)S(1)}, u32[]{:S(2)}, u32[]{:S(2)}) collective-permute-start(f32[2,1,32,384]{3,2,1,0:T(8,128)S(1)} %get-tuple-element.43), channel_id=1, source_target_pairs={{0,4},{4,8},{8,12},{1,5},{5,9},{9,13},{2,6},{6,10},{10,14},{3,7},{... | collective-permute-start | bytes 294920 | tf_op jit(solution)/shard_map/ppermute | solution.py:14
  21.4 11.3 %collective-permute-start.9 = (f32[2,1,32,384]{3,2,1,0:T(8,128)S(1)}, f32[2,1,32,384]{3,2,1,0:T(8,128)S(1)}, u32[]{:S(2)}, u32[]{:S(2)}) collective-permute-start(f32[2,1,32,384]{3,2,1,0:T(8,128)S(1)} %get-tuple-element.44), channel_id=1, source_target_pairs={{4,0},{8,4},{12,8},{5,1},{9,5},{13,9},{6,2},{10,6},{14,10},{7,3},{... | collective-permute-start | bytes 294920 | tf_op jit(solution)/shard_map/ppermute | solution.py:15
  22.7 0.7 copy-start.12
  22.7 1.4 %copy-start.13 = (f32[4]{0:T(128)S(1)}, f32[4]{0:T(128)}, u32[]{:S(2)}) copy-start(f32[4]{0:T(128)} %param.23) | copy-start | bytes 52
  26.6 11.0 %copy-start.9 = (f32[24,16,768]{2,1,0:T(8,128)S(1)}, f32[24,16,768]{2,1,0:T(8,128)}, u32[]{:S(2)}) copy-start(f32[24,16,768]{2,1,0:T(8,128)} %param.14) | copy-start | bytes 3538948
  26.7 11.0 %copy-start.8 = (f32[24,16,768]{2,1,0:T(8,128)S(1)}, f32[24,16,768]{2,1,0:T(8,128)}, u32[]{:S(2)}) copy-start(f32[24,16,768]{2,1,0:T(8,128)} %param.15) | copy-start | bytes 3538948
  26.7 11.0 %collective-permute-start.2 = (f32[26,1,768]{2,0,1:T(8,128)S(1)}, f32[26,1,768]{2,0,1:T(8,128)S(1)}, u32[]{:S(2)}, u32[]{:S(2)}) collective-permute-start(f32[26,1,768]{2,0,1:T(8,128)S(1)} %get-tuple-element.47), channel_id=1, source_target_pairs={{1,0},{2,1},{3,2},{5,4},{6,5},{7,6},{9,8},{10,9},{11,10},{13,12},{... | collective-permute-start | bytes 239624 | tf_op jit(solution)/shard_map/ppermute | solution.py:15
  28.1 9.5 %collective-permute-start.3 = (f32[26,1,768]{2,0,1:T(8,128)S(1)}, f32[26,1,768]{2,0,1:T(8,128)S(1)}, u32[]{:S(2)}, u32[]{:S(2)}) collective-permute-start(f32[26,1,768]{2,0,1:T(8,128)S(1)} %get-tuple-element.48), channel_id=1, source_target_pairs={{0,1},{1,2},{2,3},{4,5},{5,6},{6,7},{8,9},{9,10},{10,11},{12,13},{... | collective-permute-start | bytes 239624 | tf_op jit(solution)/shard_map/ppermute | solution.py:14
  32.8 15.0 %collective-permute-start.10 = (f32[2,18,1,384]{3,2,1,0:T(1,128)S(1)}, f32[2,18,1,384]{3,2,1,0:T(1,128)S(1)}, u32[]{:S(2)}, u32[]{:S(2)}) collective-permute-start(f32[2,18,1,384]{3,2,1,0:T(1,128)S(1)} %get-tuple-element.39), channel_id=1, source_target_pairs={{0,1},{1,2},{2,3},{4,5},{5,6},{6,7},{8,9},{9,10},{10,11},{12,13},{... | collective-permute-start | bytes 165896 | tf_op jit(solution)/shard_map/ppermute | solution.py:14
  36.4 11.4 %collective-permute-start.11 = (f32[2,18,1,384]{3,2,1,0:T(1,128)S(1)}, f32[2,18,1,384]{3,2,1,0:T(1,128)S(1)}, u32[]{:S(2)}, u32[]{:S(2)}) collective-permute-start(f32[2,18,1,384]{3,2,1,0:T(1,128)S(1)} %get-tuple-element.40), channel_id=1, source_target_pairs={{1,0},{2,1},{3,2},{5,4},{6,5},{7,6},{9,8},{10,9},{11,10},{13,12},{... | collective-permute-start | bytes 165896 | tf_op jit(solution)/shard_map/ppermute | solution.py:15
  43.8 4.0 %copy-start.4 = (f32[1,16,32,384]{3,2,1,0:T(8,128)S(1)}, f32[1,16,32,384]{3,2,1,0:T(8,128)}, u32[]{:S(2)}) copy-start(f32[1,16,32,384]{3,2,1,0:T(8,128)} %copy-done.3) | copy-start | bytes 2359300
  44.3 3.8 %collective-permute-start.5 = (f32[1,16,768]{2,0,1:T(1,128)S(1)}, f32[1,16,768]{2,0,1:T(1,128)S(1)}, u32[]{:S(2)}, u32[]{:S(2)}) collective-permute-start(f32[1,16,768]{2,0,1:T(1,128)S(1)} %get-tuple-element.49), channel_id=1, source_target_pairs={{0,4},{4,8},{8,12},{1,5},{5,9},{9,13},{2,6},{6,10},{10,14},{3,7},{... | collective-permute-start | bytes 147464 | tf_op jit(solution)/shard_map/ppermute | solution.py:14
  46.5 4.9 %collective-permute-start.4 = (f32[1,16,768]{2,0,1:T(1,128)S(1)}, f32[1,16,768]{2,0,1:T(1,128)S(1)}, u32[]{:S(2)}, u32[]{:S(2)}) collective-permute-start(f32[1,16,768]{2,0,1:T(1,128)S(1)} %get-tuple-element.50), channel_id=1, source_target_pairs={{4,0},{8,4},{12,8},{5,1},{9,5},{13,9},{6,2},{10,6},{14,10},{7,3},{... | collective-permute-start | bytes 147464 | tf_op jit(solution)/shard_map/ppermute | solution.py:15
  51.5 7.1 %collective-permute-start.6 = (f32[26,1,768]{2,0,1:T(8,128)S(1)}, f32[26,1,768]{2,0,1:T(8,128)S(1)}, u32[]{:S(2)}, u32[]{:S(2)}) collective-permute-start(f32[26,1,768]{2,0,1:T(8,128)S(1)} %get-tuple-element.45), channel_id=1, source_target_pairs={{1,0},{2,1},{3,2},{5,4},{6,5},{7,6},{9,8},{10,9},{11,10},{13,12},{... | collective-permute-start | bytes 239624 | tf_op jit(solution)/shard_map/ppermute | solution.py:15
  52.8 7.5 %copy-start.7 = (f32[24,16,768]{2,1,0:T(8,128)S(1)}, f32[24,16,768]{2,1,0:T(8,128)}, u32[]{:S(2)}) copy-start(f32[24,16,768]{2,1,0:T(8,128)} %param.12) | copy-start | bytes 3538948
  52.8 7.5 %copy-start.10 = (f32[24,16,768]{2,1,0:T(8,128)S(1)}, f32[24,16,768]{2,1,0:T(8,128)}, u32[]{:S(2)}) copy-start(f32[24,16,768]{2,1,0:T(8,128)} %param.16) | copy-start | bytes 3538948
  52.8 7.5 %collective-permute-start.7 = (f32[26,1,768]{2,0,1:T(8,128)S(1)}, f32[26,1,768]{2,0,1:T(8,128)S(1)}, u32[]{:S(2)}, u32[]{:S(2)}) collective-permute-start(f32[26,1,768]{2,0,1:T(8,128)S(1)} %get-tuple-element.46), channel_id=1, source_target_pairs={{0,1},{1,2},{2,3},{4,5},{5,6},{6,7},{8,9},{9,10},{10,11},{12,13},{... | collective-permute-start | bytes 239624 | tf_op jit(solution)/shard_map/ppermute | solution.py:14
  73.8 16.4 %all-to-all-start.1 = ((f32[16,6,384]{2,1,0:T(8,128)}), f32[16,6,384]{2,1,0:T(8,128)}, u32[]{:S(2)}, u32[]{:S(2)}) async-start(f32[16,6,384]{2,1,0:T(8,128)} %reshape.117), calls=%async_computation.1 | async-start | bytes 393216 | tf_op jit(solution)/shard_map/all_to_all | solution.py:110
  91.1 1.1 copy-start.1
  91.7 25.4 %copy-start.5 = (f32[16,32,384]{2,1,0:T(8,128)}, f32[16,32,384]{2,1,0:T(8,128)S(1)}, u32[]{:S(2)}) copy-start(f32[16,32,384]{2,1,0:T(8,128)S(1)} %fusion.47) | copy-start | bytes 2359300
  100.9 16.2 %copy-start.2 = (f32[16,32,384]{2,1,0:T(8,128)}, f32[16,32,384]{2,1,0:T(8,128)S(1)}, u32[]{:S(2)}) copy-start(f32[16,32,384]{2,1,0:T(8,128)S(1)} %get-tuple-element.26) | copy-start | bytes 2359300
  100.9 3.5 %collective-permute-start.12 = (f32[2,1,32,384]{3,2,1,0:T(8,128)S(1)}, f32[2,1,32,384]{3,2,1,0:T(8,128)S(1)}, u32[]{:S(2)}, u32[]{:S(2)}) collective-permute-start(f32[2,1,32,384]{3,2,1,0:T(8,128)S(1)} %get-tuple-element.41), channel_id=1, source_target_pairs={{0,4},{4,8},{8,12},{1,5},{5,9},{9,13},{2,6},{6,10},{10,14},{3,7},{... | collective-permute-start | bytes 294920 | tf_op jit(solution)/shard_map/ppermute | solution.py:14
  103.1 3.8 %collective-permute-start.13 = (f32[2,1,32,384]{3,2,1,0:T(8,128)S(1)}, f32[2,1,32,384]{3,2,1,0:T(8,128)S(1)}, u32[]{:S(2)}, u32[]{:S(2)}) collective-permute-start(f32[2,1,32,384]{3,2,1,0:T(8,128)S(1)} %get-tuple-element.42), channel_id=1, source_target_pairs={{4,0},{8,4},{12,8},{5,1},{9,5},{13,9},{6,2},{10,6},{14,10},{7,3},{... | collective-permute-start | bytes 294920 | tf_op jit(solution)/shard_map/ppermute | solution.py:15
  107.0 7.0 %collective-permute-start.14 = (f32[2,18,1,384]{3,2,1,0:T(1,128)S(1)}, f32[2,18,1,384]{3,2,1,0:T(1,128)S(1)}, u32[]{:S(2)}, u32[]{:S(2)}) collective-permute-start(f32[2,18,1,384]{3,2,1,0:T(1,128)S(1)} %get-tuple-element.37), channel_id=1, source_target_pairs={{0,1},{1,2},{2,3},{4,5},{5,6},{6,7},{8,9},{9,10},{10,11},{12,13},{... | collective-permute-start | bytes 165896 | tf_op jit(solution)/shard_map/ppermute | solution.py:14
  109.7 2.8 %copy-start.11 = (f32[24,16,768]{2,0,1:T(8,128)S(1)}, f32[24,16,768]{2,0,1:T(8,128)}, u32[]{:S(2)}) copy-start(f32[24,16,768]{2,0,1:T(8,128)} %get-tuple-element.32) | copy-start | bytes 3538948
  109.8 6.2 %collective-permute-start.15 = (f32[2,18,1,384]{3,2,1,0:T(1,128)S(1)}, f32[2,18,1,384]{3,2,1,0:T(1,128)S(1)}, u32[]{:S(2)}, u32[]{:S(2)}) collective-permute-start(f32[2,18,1,384]{3,2,1,0:T(1,128)S(1)} %get-tuple-element.38), channel_id=1, source_target_pairs={{1,0},{2,1},{3,2},{5,4},{6,5},{7,6},{9,8},{10,9},{11,10},{13,12},{... | collective-permute-start | bytes 165896 | tf_op jit(solution)/shard_map/ppermute | solution.py:15
where the time goes:
time: 127 us; the launch traced here: 124 us
  starting transfers between devices  53.6 us (42%)
  other arithmetic  33.3 us (26%)
  local copies, waits for them, and re-layouts  18.1 us (14%)
  waiting for transfers between devices  15.6 us (12%)
  matrix products  2.46 us (2%)
    ppermute x8, starting transfers between devices, extended(): before = lax.ppermute(last, axis, up)  27.4 us
    ppermute x8, starting transfers between devices, extended(): after = lax.ppermute(first, axis, down)  10.6 us
    another operation x2, other arithmetic, elastic_step(): ext = extended(jnp.stack([now, now - before]), (('gx', 1), ('gy', 2)), 1)  10.1 us
    all_to_all x1, starting transfers between devices, local(): lax.all_to_all(send_lines.reshape(blocks, capacity, lateral // 2), ('gx',...  8.29 us
    ppermute x8, waiting for transfers between devices, extended(): after = lax.ppermute(first, axis, down)  8.15 us
    all_to_all x1, starting transfers between devices, local(): lax.all_to_all(send_places.reshape(blocks, capacity), ('gx', 'gy'), split...  7.39 us
    add x1, other arithmetic, elastic_step(): 2.0 * now - before + shear * laplace_ext(ext[0])  7.28 us
    sub x1, other arithmetic, wave_update(): 2.0 * now - before + courant * laplace_ext(now_ext)  6.11 us
  transfers between devices with their start and end apart: 18, of which 6 were waited for; matrix products, arithmetic and copies ran while one was open for 15% of the time, Pallas kernels for 0%

commit v1 on v0

v1 whole, which is shorter than its diff:
```python
import functools

import jax
import jax.numpy as jnp
from jax import lax
from jax.experimental import pallas as pl
from jax.experimental.pallas import tpu as pltpu
from jax.sharding import PartitionSpec as P

MESH = pl.DeviceIdType.MESH
F32 = jnp.float32
BF16 = jnp.bfloat16


def iota(shape, dim):
    return lax.broadcasted_iota(jnp.int32, shape, dim)


def split(x):
    high = x.astype(BF16)
    low = (x - high.astype(F32)).astype(BF16)
    return high, low


def dot(a, b):
    return jnp.dot(a, b, preferred_element_type=F32)


def laplace(centre, up, down, left, right):
    rows, lanes = centre.shape
    row, lane = iota(centre.shape, 0), iota(centre.shape, 1)
    xm = jnp.where(row == 0, left, pltpu.roll(centre, 1, 0))
    xp = jnp.where(row == rows - 1, right, pltpu.roll(centre, rows - 1, 0))
    ym = jnp.where(lane == 0, 0.0, pltpu.roll(centre, 1, 1))
    yp = jnp.where(lane == lanes - 1, 0.0, pltpu.roll(centre, lanes - 1, 1))
    return ((up + down) + (xm + xp)) + ((ym + yp) - 6.0 * centre)


class Faces:
    def __init__(self, axis, first, last, halo, send, recv, base):
        size, index = lax.axis_size(axis), lax.axis_index(axis)
        self.halo = halo
        self.has_next, self.has_prev = index < size - 1, index > 0
        self.up = pltpu.make_async_remote_copy(
            src_ref=last, dst_ref=halo.at[0], send_sem=send.at[base], recv_sem=recv.at[base],
            device_id={axis: lax.rem(index + 1, size)}, device_id_type=MESH)
        self.down = pltpu.make_async_remote_copy(
            src_ref=first, dst_ref=halo.at[1], send_sem=send.at[base + 1], recv_sem=recv.at[base + 1],
            device_id={axis: lax.rem(index + size - 1, size)}, device_id_type=MESH)

    def clear(self):
        @pl.when(jnp.logical_not(self.has_prev))
        def _():
            self.halo[0] = jnp.zeros(self.halo.shape[1:], F32)

        @pl.when(jnp.logical_not(self.has_next))
        def _():
            self.halo[1] = jnp.zeros(self.halo.shape[1:], F32)

    def start(self):
        pl.when(self.has_next)(self.up.start)
        pl.when(self.has_prev)(self.down.start)

    def wait(self):
        pl.when(self.has_prev)(self.up.wait_recv)
        pl.when(self.has_next)(self.down.wait_recv)

    def wait_send(self):
        pl.when(self.has_next)(self.up.wait_send)
        pl.when(self.has_prev)(self.down.wait_send)


def kernel(
    capacity, slots,
    p_in, q_in, c_in, n_in, a_in, own, slot, u_in, w_in, k_in, shear_table, viscosity_table,
    pm, pn, tf, um, un,
    p, q, c, n, a, u, w, k, load,
    hz_p, hx_p, fx_p, hz_m, hx_m, fx_m,
    hz_u, hx_u, fx_u, hz_w, hx_w, fx_w, hz_e, hx_e, fx_e,
    rest, both, paired, packed, got, packed_places, got_places,
    send, recv, line_send, line_recv, place_send, place_recv,
):
    planes, rows, lateral = p.shape
    tile_rows, tile_cols, tile_depth = u.shape
    kinds = shear_table.shape[0]
    gx, gy = lax.axis_size("gx"), lax.axis_size("gy")
    blocks = gx * gy
    me = lax.axis_index("gx") * gy + lax.axis_index("gy")

    loads = [pltpu.make_async_copy(s, d, load.at[i]) for i, (s, d) in enumerate(
        ((p_in, p), (u_in, u), (w_in, w), (q_in, q), (c_in, c), (n_in, n), (a_in, a), (k_in, k)))]
    for copy in loads:
        copy.start()

    barrier = pltpu.get_barrier_semaphore()

    def greet(d, carry):
        other = lax.rem(me + d, blocks)
        pl.semaphore_signal(
            barrier, inc=1, device_id={"gx": other // gy, "gy": lax.rem(other, gy)}, device_id_type=MESH)
        return carry

    lax.fori_loop(1, blocks, greet, 0)

    def faces(first, last, halo, axis, base):
        return Faces(axis, first, last, halo, send, recv, base)

    def pair(field, hz, fx, hx, base):
        depth = field.shape[0]
        return (faces(field.at[0], field.at[depth - 1], hz, "gx", base),
                faces(fx.at[0], fx.at[1], hx, "gy", base + 2))

    p_z, p_x = pair(p, hz_p, fx_p, hx_p, 0)
    m_z, m_x = pair(pm, hz_m, fx_m, hx_m, 4)
    u_z, u_x = pair(u, hz_u, fx_u, hx_u, 8)
    w_z, w_x = pair(w, hz_w, fx_w, hx_w, 12)
    e_z, e_x = pair(um, hz_e, fx_e, hx_e, 16)
    every = (p_z, p_x, m_z, m_x, u_z, u_x, w_z, w_x, e_z, e_x)
    for item in every:
        item.clear()

    def stage(field, fx):
        def body(z, carry):
            plane = field[z]
            fx[0, pl.ds(z, 1), :] = plane[:1]
            fx[1, pl.ds(z, 1), :] = plane[-1:]
            return carry
        lax.fori_loop(0, field.shape[0], body, 0)

    loads[0].wait()
    stage(p, fx_p)
    pl.semaphore_wait(barrier, blocks - 1)
    p_z.start()
    p_x.start()
    loads[1].wait()
    loads[2].wait()
    stage(u, fx_u)
    stage(w, fx_w)
    u_z.start()
    u_x.start()
    w_z.start()
    w_x.start()

    lines_z, lines_x = own.shape
    count = lines_z * rows

    def along_lanes(table):
        column = iota((lines_z, count), 1)
        line_z, line_x = iota((lines_z, count), 0), lax.rem(column, rows) // 2
        here = line_z == column // rows
        total = jnp.zeros((lines_z, count), F32)
        for b in range(lines_x):
            total = total + jnp.where(here & (line_x == b), table[:, b:b + 1], 0.0)
        return jnp.sum(total, axis=0, keepdims=True)

    def along_rows(table):
        spread = jnp.concatenate(
            [jnp.broadcast_to(table[z:z + 1], (rows, lines_x)) for z in range(lines_z)], axis=0)
        row, line_x = iota((count, lines_x), 0), iota((count, lines_x), 1)
        return jnp.sum(jnp.where(line_x == lax.rem(row, rows) // 2, spread, 0.0), axis=1, keepdims=True)

    owners = own[...].astype(F32)
    owner_lane, owner_row = along_lanes(owners), along_rows(owners)
    place_lane = along_lanes(slot[...].astype(F32))
    earlier = iota((count, count), 0) // 2 < iota((count, count), 1) // 2
    rank = 0.5 * jnp.sum(
        jnp.where((owner_row == owner_lane) & earlier, 1.0, 0.0), axis=0, keepdims=True)
    target = owner_lane * float(slots) + rank
    match = iota((blocks * slots, count), 0).astype(F32) == target
    even = lax.rem(iota((blocks * slots, count), 1), 2) == 0
    places = jnp.sum(jnp.where(match & even, place_lane + 1.0, 0.0), axis=1, keepdims=True)
    packed_places[...] = jnp.broadcast_to(places, packed_places.shape)
    match = jnp.where(match, 1.0, 0.0).astype(BF16)

    def sends(source, target_ref, send_sems, recv_sems):
        def copy(d):
            other = lax.rem(me + d, blocks)
            return pltpu.make_async_remote_copy(
                src_ref=source.at[pl.ds(pl.multiple_of(other * slots, slots), slots)],
                dst_ref=target_ref.at[pl.ds(pl.multiple_of(me * slots, slots), slots)],
                send_sem=send_sems.at[d], recv_sem=recv_sems.at[d],
                device_id={"gx": other // gy, "gy": lax.rem(other, gy)}, device_id_type=MESH)

        def start():
            lax.fori_loop(1, blocks, lambda d, carry: (copy(d).start(), carry)[1], 0)
            here = pl.ds(pl.multiple_of(me * slots, slots), slots)
            target_ref[here, :] = source[here, :]

        def wait():
            lax.fori_loop(1, blocks, lambda d, carry: (copy(d).wait_recv(), carry)[1], 0)

        def wait_send():
            lax.fori_loop(1, blocks, lambda d, carry: (copy(d).wait_send(), carry)[1], 0)

        return start, wait, wait_send

    start_places, wait_places, wait_places_send = sends(packed_places, got_places, place_send, place_recv)
    start_lines, wait_lines, wait_lines_send = sends(packed, got, line_send, line_recv)
    start_places()

    def wave(now, before, lap, z):
        return (2.0 * now - before + c[z] * lap + n[z] * (now * now - before * before)
                - 0.1 * a[z] * (now - before))

    def first(z, up, down):
        now = p[z]
        lap = laplace(now, up, down, hx_p[0, pl.ds(z, 1), :], hx_p[1, pl.ds(z, 1), :])
        mid = wave(now, q[z], lap, z)
        pm[z] = mid
        fx_m[0, pl.ds(z, 1), :] = mid[:1]
        fx_m[1, pl.ds(z, 1), :] = mid[-1:]

    for copy in loads[3:7]:
        copy.wait()
    p_z.wait()
    p_x.wait()
    first(0, hz_p[0], p[1])
    first(planes - 1, p[planes - 2], hz_p[1])
    m_z.start()
    lax.fori_loop(1, planes - 1, lambda z, carry: (first(z, p[z - 1], p[z + 1]), carry)[1], 0)
    m_x.start()

    loads[7].wait()
    for item in (u_z, u_x, w_z, w_x):
        item.wait()

    def elastic(z, u_up, u_down, w_up, w_down):
        now, before, kind = u[z], w[z], k[z]
        lap_u = laplace(now, u_up, u_down, hx_u[0, pl.ds(z, 1), :], hx_u[1, pl.ds(z, 1), :])
        lap_w = laplace(before, w_up, w_down, hx_w[0, pl.ds(z, 1), :], hx_w[1, pl.ds(z, 1), :])
        shear, viscosity = jnp.zeros(now.shape, F32), jnp.zeros(now.shape, F32)
        for i in range(kinds):
            shear = jnp.where(kind == i, shear_table[i], shear)
            viscosity = jnp.where(kind == i, viscosity_table[i], viscosity)
        um[z] = 2.0 * now - before + shear * lap_u + viscosity * (lap_u - lap_w)
        rest[z] = now + viscosity * lap_u
        both[z] = shear + viscosity

    elastic(0, hz_u[0], u[1], hz_w[0], w[1])
    elastic(tile_rows - 1, u[tile_rows - 2], hz_u[1], w[tile_rows - 2], hz_w[1])
    lax.fori_loop(1, tile_rows - 1, lambda z, carry: (
        elastic(z, u[z - 1], u[z + 1], w[z - 1], w[z + 1]), carry)[1], 0)

    def second(z, up, down):
        now = pm[z]
        lap = laplace(now, up, down, hx_m[0, pl.ds(z, 1), :], hx_m[1, pl.ds(z, 1), :])
        new = wave(now, p[z], lap, z)
        pn[z] = new
        return 0.1 * a[z] * (now * now + new * new) * lax.rsqrt(c[z])

    def pair_at(i):
        return pl.ds(pl.multiple_of(i * rows, rows), rows)

    m_z.wait()
    m_x.wait()
    paired[pair_at(0), :] = second(0, hz_m[0], pm[1]) + second(1, pm[0], pm[2])
    last = planes // 2 - 1
    paired[pair_at(last), :] = second(planes - 2, pm[planes - 3], pm[planes - 1]) + second(
        planes - 1, pm[planes - 2], hz_m[1])

    def two(i, carry):
        z = 2 * i
        paired[pair_at(i), :] = second(z, pm[z - 1], pm[z + 1]) + second(z + 1, pm[z], pm[z + 2])
        return carry

    lax.fori_loop(1, last, two, 0)

    width = 256
    half = width // 2
    lanes_two = jnp.where(iota((width, half), 0) // 2 == iota((width, half), 1), 0.125, 0.0).astype(BF16)
    for i in range(lateral // width):
        high, low = split(paired[:, i * width:(i + 1) * width])
        coarse = dot(high, lanes_two) + dot(low, lanes_two)
        high, low = split(coarse)
        packed[:, i * half:(i + 1) * half] = dot(match, high) + dot(match, low)
    start_lines()

    wait_places()
    spots = jnp.transpose(got_places[...])[:1] - 1.0
    cells = tile_rows * tile_cols
    landing = jnp.where(
        iota((cells, blocks * slots), 0).astype(F32) == spots, 1.0, 0.0).astype(BF16)
    wait_lines()
    high, low = split(got[...])
    chunk = 4 if tile_rows % 4 == 0 else 1
    for r in range(0, tile_rows, chunk):
        part = landing[r * tile_cols:(r + chunk) * tile_cols]
        force = (dot(part, high) + dot(part, low)).reshape(chunk, tile_cols, tile_depth)
        tf[r:r + chunk] = force
        mid = um[r:r + chunk] + 0.25 * force
        um[r:r + chunk] = mid
        for j in range(chunk):
            fx_e[0, r + j:r + j + 1, :] = mid[j, :1]
            fx_e[1, r + j:r + j + 1, :] = mid[j, -1:]
    e_z.start()
    e_x.start()
    e_z.wait()
    e_x.wait()

    def final(z, up, down):
        now = um[z]
        lap = laplace(now, up, down, hx_e[0, pl.ds(z, 1), :], hx_e[1, pl.ds(z, 1), :])
        un[z] = 2.0 * now - rest[z] + both[z] * lap + 0.25 * tf[z]

    final(0, hz_e[0], um[1])
    final(tile_rows - 1, um[tile_rows - 2], hz_e[1])
    lax.fori_loop(1, tile_rows - 1, lambda z, carry: (final(z, um[z - 1], um[z + 1]), carry)[1], 0)
    for item in every:
        item.wait_send()
    wait_places_send()
    wait_lines_send()


def local(pressure, pressure_prev, courant, nonlinearity, absorption, own_map, slot_table,
          displacement, displacement_prev, layer_labels, shear_table, viscosity_table):
    planes, rows, lateral = pressure.shape
    tile = displacement.shape
    blocks = lax.axis_size("gx") * lax.axis_size("gy")
    capacity = max(2, own_map.shape[0] * own_map.shape[1] // blocks)
    slots = -(-capacity // 8) * 8
    anywhere = pl.BlockSpec(memory_space=pl.ANY)
    vmem = pl.BlockSpec(memory_space=pltpu.VMEM)
    smem = pl.BlockSpec(memory_space=pltpu.SMEM)
    wave, cell = pltpu.VMEM(pressure.shape, F32), pltpu.VMEM(tile, F32)

    def halos(shape):
        z, x = pltpu.VMEM((2,) + shape[1:], F32), pltpu.VMEM((2, shape[0], shape[2]), F32)
        return [z, x, x]

    dma = pltpu.SemaphoreType.DMA
    return pl.pallas_call(
        functools.partial(kernel, capacity, slots),
        out_shape=[jax.ShapeDtypeStruct(pressure.shape, F32)] * 2 + [jax.ShapeDtypeStruct(tile, F32)] * 3,
        in_specs=[anywhere] * 5 + [vmem] * 2 + [anywhere] * 3 + [smem] * 2,
        out_specs=[vmem] * 5,
        scratch_shapes=[wave] * 5 + [cell] * 2 + [pltpu.VMEM(tile, jnp.int32), dma((8,))]
        + halos(pressure.shape) * 2 + halos(tile) * 3
        + [cell, cell,
           pltpu.VMEM((planes // 2 * rows, lateral), F32),
           pltpu.VMEM((blocks * slots, lateral // 2), F32),
           pltpu.VMEM((blocks * slots, lateral // 2), F32),
           pltpu.VMEM((blocks * slots, 128), F32),
           pltpu.VMEM((blocks * slots, 128), F32),
           dma((20,)), dma((20,)), dma((blocks,)), dma((blocks,)), dma((blocks,)), dma((blocks,))],
        compiler_params=pltpu.CompilerParams(
            collective_id=0, has_side_effects=True, vmem_limit_bytes=40 * 1024 * 1024),
    )(pressure, pressure_prev, courant, nonlinearity, absorption, own_map, slot_table,
      displacement, displacement_prev, layer_labels, shear_table, viscosity_table)


def solution(mesh):
    field = P(("group", "gx"), "gy", None)
    table = P(("group", "gx"), "gy")
    return jax.shard_map(
        local,
        mesh=mesh,
        in_specs=(field,) * 5 + (table,) * 2 + (field,) * 3 + (P("group"),) * 2,
        out_specs=(field,) * 5,
        check_vma=False,
    )
```

time: 127 us -> 49.8 us (0.39); the launches traced: 124 us -> 49.3 us
  starting transfers between devices: 53.6 us -> 0 us
  other arithmetic: 33.3 us -> 0 us
  Pallas kernels: 0 us -> 31.4 us
  waiting for transfers between devices: 15.6 us -> 0 us
  matrix products: 2.46 us -> 0 us
    ppermute x16 -> x0, starting transfers between devices: 38 us -> none  [the longest x8 27.4 us: extended(): before = lax.ppermute(last, axis, up)]
    pallas_call x0 -> x1, Pallas kernels: none -> 31.4 us  [local(): pl.pallas_call(functools.partial(kernel, capacity, slots), out_shape=[jax...]
    all_to_all x2 -> x0, starting transfers between devices: 15.7 us -> none  [the longest x1 8.29 us: local(): lax.all_to_all(send_lines.reshape(blocks, capacity, lateral // 2), ('gx',...]
    unnamed x32 -> x27, local copies, waits for them, and re-layouts: 4.89 us -> 17.3 us
    another operation x2 -> x0, other arithmetic: 10.1 us -> none  [elastic_step(): ext = extended(jnp.stack([now, now - before]), (('gx', 1), ('gy', 2)), 1)]
    ppermute x16 -> x0, waiting for transfers between devices: 9.86 us -> none  [the longest x8 8.15 us: extended(): after = lax.ppermute(first, axis, down)]
    add x3 -> x0, other arithmetic: 7.98 us -> none  [the longest x1 7.28 us: elastic_step(): 2.0 * now - before + shear * laplace_ext(ext[0])]
    slice x11 -> x0, local copies, waits for them, and re-layouts: 7.35 us -> none  [the longest x5 5.07 us: laplace_ext(): upper = jnp.concatenate([centre[:, :, 1:], zeros], axis=2)]
  transfers between devices with their start and end apart: 18 -> 0, of which waited for: 6 -> 0; matrix products, arithmetic and copies ran while one was open for 15% -> 0% of each run, Pallas kernels for 0% -> 0%
where the time goes in v1:
time: 49.8 us; the launch traced here: 49.3 us
  Pallas kernels  31.4 us (63%)
  local copies, waits for them, and re-layouts  17.3 us (35%)
  between operations  0.65 us (1%)
    pallas_call x1, Pallas kernels, local(): pl.pallas_call(functools.partial(kernel, capacity, slots), out_shape=[jax...  31.4 us
    unnamed x27, local copies, waits for them, and re-layouts  17.3 us

profile of v1, /device:TPU:0, one launch (start us, length us, event | category | flops | bytes accessed | tf_op | source)
XLA Modules:
  0.0 49.3 jit_solution(11114854453145898080)
XLA Ops:
  0.6 0.8 %copy.17.own = s32[12,8]{1,0:T(8,128)S(1)} copy(s32[12,8]{0,1:T(8,128)} %param.17) | data formatting | bytes 768 | tf_op args[5]
  1.4 0.8 %copy.18.slot = s32[12,8]{1,0:T(8,128)S(1)} copy(s32[12,8]{0,1:T(8,128)} %param.18) | data formatting | bytes 768 | tf_op args[6]
  2.2 0.0 copy-start
  2.2 1.3 %copy-done = f32[24,16,768]{2,1,0:T(8,128)S(1)} copy-done((f32[24,16,768]{2,1,0:T(8,128)S(1)}, f32[24,16,768]{2,1,0:T(8,128)}, u32[]{:S(2)}) %copy-start) | copy-done | bytes 1179672
  3.4 0.0 copy-start.1
  3.4 1.3 %copy-done.1 = f32[24,16,768]{2,1,0:T(8,128)S(1)} copy-done((f32[24,16,768]{2,1,0:T(8,128)S(1)}, f32[24,16,768]{2,1,0:T(8,128)}, u32[]{:S(2)}) %copy-start.1) | copy-done | bytes 1179672
  4.7 0.0 copy-start.2
  4.7 1.3 %copy-done.2 = f32[24,16,768]{2,1,0:T(8,128)S(1)} copy-done((f32[24,16,768]{2,1,0:T(8,128)S(1)}, f32[24,16,768]{2,1,0:T(8,128)}, u32[]{:S(2)}) %copy-start.2) | copy-done | bytes 1179672
  6.0 0.0 copy-start.3
  6.0 1.3 %copy-done.3 = f32[24,16,768]{2,1,0:T(8,128)S(1)} copy-done((f32[24,16,768]{2,1,0:T(8,128)S(1)}, f32[24,16,768]{2,1,0:T(8,128)}, u32[]{:S(2)}) %copy-start.3) | copy-done | bytes 1179672
  7.3 0.0 copy-start.4
  7.3 1.3 %copy-done.4 = f32[24,16,768]{2,1,0:T(8,128)S(1)} copy-done((f32[24,16,768]{2,1,0:T(8,128)S(1)}, f32[24,16,768]{2,1,0:T(8,128)}, u32[]{:S(2)}) %copy-start.4) | copy-done | bytes 1179672
  8.5 0.0 copy-start.5
  8.5 1.1 %copy-done.5 = f32[16,32,384]{2,1,0:T(8,128)S(1)} copy-done((f32[16,32,384]{2,1,0:T(8,128)S(1)}, f32[16,32,384]{2,1,0:T(8,128)}, u32[]{:S(2)}) %copy-start.5) | copy-done | bytes 786456
  9.7 0.0 copy-start.6
  9.7 1.1 %copy-done.6 = f32[16,32,384]{2,1,0:T(8,128)S(1)} copy-done((f32[16,32,384]{2,1,0:T(8,128)S(1)}, f32[16,32,384]{2,1,0:T(8,128)}, u32[]{:S(2)}) %copy-start.6) | copy-done | bytes 786456
  10.8 0.0 copy-start.7
  10.8 1.1 %copy-done.7 = s32[16,32,384]{2,1,0:T(8,128)S(1)} copy-done((s32[16,32,384]{2,1,0:T(8,128)S(1)}, s32[16,32,384]{2,1,0:T(8,128)}, u32[]{:S(2)}) %copy-start.7) | copy-done | bytes 786456
  11.9 0.0 copy-start.8
  11.9 0.7 %copy-done.8 = f32[4]{0:T(128)S(1)} copy-done((f32[4]{0:T(128)S(1)}, f32[4]{0:T(128)}, u32[]{:S(2)}) %copy-start.8) | copy-done | bytes 40
  12.6 0.0 copy-start.9
  12.6 0.7 %copy-done.9 = f32[4]{0:T(128)S(1)} copy-done((f32[4]{0:T(128)S(1)}, f32[4]{0:T(128)}, u32[]{:S(2)}) %copy-start.9) | copy-done | bytes 40
  13.2 31.4 %shard_map.155 = (f32[24,16,768]{2,1,0:T(8,128)S(1)}, f32[24,16,768]{2,1,0:T(8,128)S(1)}, f32[16,32,384]{2,1,0:T(8,128)S(1)}, f32[16,32,384]{2,1,0:T(8,128)S(1)}, f32[16,32,384]{2,1,0:T(8,128)S(1)}) custom-call(f32[24,16,768]{2,1,0:T(8,128)S(1)} %copy-done, f32[24,16,768]{2,1,0:T(8,128)S(1)} %copy-done.1, f32[24,16,768]{2,1,0:T(8,128)S(1)} %copy-done.2, ...), custom_call_target="tpu_custom_call" | custom-call | tf_op jit(solution)/shard_map/pallas_call | solution.py:331
  44.6 1.0 %copy.24 = f32[24,16,768]{2,1,0:T(8,128)} copy(f32[24,16,768]{2,1,0:T(8,128)S(1)} %get-tuple-element.10) | data formatting | bytes 2359296
  45.6 1.0 %copy.25 = f32[24,16,768]{2,1,0:T(8,128)} copy(f32[24,16,768]{2,1,0:T(8,128)S(1)} %get-tuple-element.11) | data formatting | bytes 2359296
  46.6 0.9 %copy.26 = f32[16,32,384]{2,1,0:T(8,128)} copy(f32[16,32,384]{2,1,0:T(8,128)S(1)} %get-tuple-element.12) | data formatting | bytes 1572864
  47.5 0.9 %copy.27 = f32[16,32,384]{2,1,0:T(8,128)} copy(f32[16,32,384]{2,1,0:T(8,128)S(1)} %get-tuple-element.13) | data formatting | bytes 1572864
  48.4 0.9 %copy.28 = f32[16,32,384]{2,1,0:T(8,128)} copy(f32[16,32,384]{2,1,0:T(8,128)S(1)} %get-tuple-element.14) | data formatting | bytes 1572864
Async XLA Ops:
  2.2 1.3 %copy-start = (f32[24,16,768]{2,1,0:T(8,128)S(1)}, f32[24,16,768]{2,1,0:T(8,128)}, u32[]{:S(2)}) copy-start(f32[24,16,768]{2,1,0:T(8,128)} %p_in.1) | copy-start | bytes 3538948
  3.4 1.3 %copy-start.1 = (f32[24,16,768]{2,1,0:T(8,128)S(1)}, f32[24,16,768]{2,1,0:T(8,128)}, u32[]{:S(2)}) copy-start(f32[24,16,768]{2,1,0:T(8,128)} %q_in.1) | copy-start | bytes 3538948
  4.7 1.3 %copy-start.2 = (f32[24,16,768]{2,1,0:T(8,128)S(1)}, f32[24,16,768]{2,1,0:T(8,128)}, u32[]{:S(2)}) copy-start(f32[24,16,768]{2,1,0:T(8,128)} %c_in.1) | copy-start | bytes 3538948
  6.0 1.3 %copy-start.3 = (f32[24,16,768]{2,1,0:T(8,128)S(1)}, f32[24,16,768]{2,1,0:T(8,128)}, u32[]{:S(2)}) copy-start(f32[24,16,768]{2,1,0:T(8,128)} %n_in.1) | copy-start | bytes 3538948
  7.3 1.3 %copy-start.4 = (f32[24,16,768]{2,1,0:T(8,128)S(1)}, f32[24,16,768]{2,1,0:T(8,128)}, u32[]{:S(2)}) copy-start(f32[24,16,768]{2,1,0:T(8,128)} %a_in.1) | copy-start | bytes 3538948
  8.5 1.1 %copy-start.5 = (f32[16,32,384]{2,1,0:T(8,128)S(1)}, f32[16,32,384]{2,1,0:T(8,128)}, u32[]{:S(2)}) copy-start(f32[16,32,384]{2,1,0:T(8,128)} %u_in.1) | copy-start | bytes 2359300
  9.7 1.1 %copy-start.6 = (f32[16,32,384]{2,1,0:T(8,128)S(1)}, f32[16,32,384]{2,1,0:T(8,128)}, u32[]{:S(2)}) copy-start(f32[16,32,384]{2,1,0:T(8,128)} %w_in.1) | copy-start | bytes 2359300
  10.8 1.1 %copy-start.7 = (s32[16,32,384]{2,1,0:T(8,128)S(1)}, s32[16,32,384]{2,1,0:T(8,128)}, u32[]{:S(2)}) copy-start(s32[16,32,384]{2,1,0:T(8,128)} %k_in.1) | copy-start | bytes 2359300
  11.9 0.7 %copy-start.8 = (f32[4]{0:T(128)S(1)}, f32[4]{0:T(128)}, u32[]{:S(2)}) copy-start(f32[4]{0:T(128)} %shear_table.1) | copy-start | bytes 52
  12.6 0.7 %copy-start.9 = (f32[4]{0:T(128)S(1)}, f32[4]{0:T(128)}, u32[]{:S(2)}) copy-start(f32[4]{0:T(128)} %viscosity_table.1) | copy-start | bytes 52

commit v2 on v1

--- a/solution.py
+++ b/solution.py
@@ -72,12 +72,12 @@
 
 def kernel(
     capacity, slots,
-    p_in, q_in, c_in, n_in, a_in, own, slot, u_in, w_in, k_in, shear_table, viscosity_table,
-    pm, pn, tf, um, un,
-    p, q, c, n, a, u, w, k, load,
+    p_in, q_in, c_in, n_in, a_in, own_in, slot_in, u_in, w_in, k_in, shear_in, viscosity_in,
+    pm, pn, tf, um, rest, both, hz_out, hx_out,
+    p, q, c, n, a, u, w, k, own, slot, shear_table, viscosity_table, load,
     hz_p, hx_p, fx_p, hz_m, hx_m, fx_m,
     hz_u, hx_u, fx_u, hz_w, hx_w, fx_w, hz_e, hx_e, fx_e,
-    rest, both, paired, packed, got, packed_places, got_places,
+    paired, packed, got, packed_places, got_places,
     send, recv, line_send, line_recv, place_send, place_recv,
 ):
     planes, rows, lateral = p.shape
@@ -88,7 +88,8 @@
     me = lax.axis_index("gx") * gy + lax.axis_index("gy")
 
     loads = [pltpu.make_async_copy(s, d, load.at[i]) for i, (s, d) in enumerate(
-        ((p_in, p), (u_in, u), (w_in, w), (q_in, q), (c_in, c), (n_in, n), (a_in, a), (k_in, k)))]
+        ((p_in, p), (u_in, u), (w_in, w), (own_in, own), (slot_in, slot), (shear_in, shear_table),
+         (viscosity_in, viscosity_table), (q_in, q), (c_in, c), (n_in, n), (a_in, a), (k_in, k)))]
     for copy in loads:
         copy.start()
 
@@ -141,27 +142,26 @@
     w_z.start()
     w_x.start()
 
-    lines_z, lines_x = own.shape
+    loads[3].wait()
+    loads[4].wait()
+
+    lines_x, lines_z = own.shape
     count = lines_z * rows
+    padded = -(-count // 128) * 128
 
     def along_lanes(table):
-        column = iota((lines_z, count), 1)
-        line_z, line_x = iota((lines_z, count), 0), lax.rem(column, rows) // 2
-        here = line_z == column // rows
-        total = jnp.zeros((lines_z, count), F32)
-        for b in range(lines_x):
-            total = total + jnp.where(here & (line_x == b), table[:, b:b + 1], 0.0)
+        column = iota((lines_x, padded), 1)
+        here = lax.rem(column, rows) // 2 == iota((lines_x, padded), 0)
+        total = jnp.zeros((lines_x, padded), F32)
+        for z in range(lines_z):
+            total = total + jnp.where(here & (column // rows == z), table[:, z:z + 1], 0.0)
         return jnp.sum(total, axis=0, keepdims=True)
 
-    def along_rows(table):
-        spread = jnp.concatenate(
-            [jnp.broadcast_to(table[z:z + 1], (rows, lines_x)) for z in range(lines_z)], axis=0)
-        row, line_x = iota((count, lines_x), 0), iota((count, lines_x), 1)
-        return jnp.sum(jnp.where(line_x == lax.rem(row, rows) // 2, spread, 0.0), axis=1, keepdims=True)
-
     owners = own[...].astype(F32)
-    owner_lane, owner_row = along_lanes(owners), along_rows(owners)
-    place_lane = along_lanes(slot[...].astype(F32))
+    owner_lane = along_lanes(owners)
+    owner_row = jnp.transpose(jnp.broadcast_to(owner_lane, (128, padded)))[:count, :1]
+    owner_lane = owner_lane[:, :count]
+    place_lane = along_lanes(slot[...].astype(F32))[:, :count]
     earlier = iota((count, count), 0) // 2 < iota((count, count), 1) // 2
     rank = 0.5 * jnp.sum(
         jnp.where((owner_row == owner_lane) & earlier, 1.0, 0.0), axis=0, keepdims=True)
@@ -210,7 +210,7 @@
         fx_m[0, pl.ds(z, 1), :] = mid[:1]
         fx_m[1, pl.ds(z, 1), :] = mid[-1:]
 
-    for copy in loads[3:7]:
+    for copy in loads[7:11]:
         copy.wait()
     p_z.wait()
     p_x.wait()
@@ -220,7 +220,9 @@
     lax.fori_loop(1, planes - 1, lambda z, carry: (first(z, p[z - 1], p[z + 1]), carry)[1], 0)
     m_x.start()
 
-    loads[7].wait()
+    loads[5].wait()
+    loads[6].wait()
+    loads[11].wait()
     for item in (u_z, u_x, w_z, w_x):
         item.wait()
 
@@ -297,18 +299,33 @@
     e_z.wait()
     e_x.wait()
 
-    def final(z, up, down):
-        now = um[z]
-        lap = laplace(now, up, down, hx_e[0, pl.ds(z, 1), :], hx_e[1, pl.ds(z, 1), :])
-        un[z] = 2.0 * now - rest[z] + both[z] * lap + 0.25 * tf[z]
-
-    final(0, hz_e[0], um[1])
-    final(tile_rows - 1, um[tile_rows - 2], hz_e[1])
-    lax.fori_loop(1, tile_rows - 1, lambda z, carry: (final(z, um[z - 1], um[z + 1]), carry)[1], 0)
+    hz_out[...] = hz_e[...]
+    hx_out[...] = hx_e[...]
     for item in every:
         item.wait_send()
     wait_places_send()
     wait_lines_send()
+
+
+def finish(pm, pn, tf, um, rest, both, hz, hx, pm_out, pn_out, tf_out, um_out, un_out, un, sems):
+    copies = [pltpu.make_async_copy(s, d, sems.at[i]) for i, (s, d) in enumerate(
+        ((pm, pm_out), (pn, pn_out), (tf, tf_out), (um, um_out)))]
+    for copy in copies:
+        copy.start()
+    tile_rows = um.shape[0]
+
+    def final(z, up, down):
+        now = um[z]
+        lap = laplace(now, up, down, hx[0, pl.ds(z, 1), :], hx[1, pl.ds(z, 1), :])
+        un[z] = 2.0 * now - rest[z] + both[z] * lap + 0.25 * tf[z]
+
+    final(0, hz[0], um[1])
+    final(tile_rows - 1, um[tile_rows - 2], hz[1])
+    lax.fori_loop(1, tile_rows - 1, lambda z, carry: (final(z, um[z - 1], um[z + 1]), carry)[1], 0)
+    copies.append(pltpu.make_async_copy(un, un_out, sems.at[4]))
+    copies[4].start()
+    for copy in copies:
+        copy.wait()
 
 
 def local(pressure, pressure_prev, courant, nonlinearity, absorption, own_map, slot_table,
@@ -318,9 +335,8 @@
     blocks = lax.axis_size("gx") * lax.axis_size("gy")
     capacity = max(2, own_map.shape[0] * own_map.shape[1] // blocks)
     slots = -(-capacity // 8) * 8
-    anywhere = pl.BlockSpec(memory_space=pl.ANY)
+    hbm = pl.BlockSpec(memory_space=pltpu.HBM)
     vmem = pl.BlockSpec(memory_space=pltpu.VMEM)
-    smem = pl.BlockSpec(memory_space=pltpu.SMEM)
     wave, cell = pltpu.VMEM(pressure.shape, F32), pltpu.VMEM(tile, F32)
 
     def halos(shape):
@@ -328,24 +344,38 @@
         return [z, x, x]
 
     dma = pltpu.SemaphoreType.DMA
-    return pl.pallas_call(
+    kinds = shear_table.shape[0]
+    lines = pltpu.VMEM(own_map.shape[::-1], jnp.int32)
+    waves = [jax.ShapeDtypeStruct(pressure.shape, F32)] * 2
+    cells = [jax.ShapeDtypeStruct(tile, F32)]
+    parts = pl.pallas_call(
         functools.partial(kernel, capacity, slots),
-        out_shape=[jax.ShapeDtypeStruct(pressure.shape, F32)] * 2 + [jax.ShapeDtypeStruct(tile, F32)] * 3,
-        in_specs=[anywhere] * 5 + [vmem] * 2 + [anywhere] * 3 + [smem] * 2,
-        out_specs=[vmem] * 5,
-        scratch_shapes=[wave] * 5 + [cell] * 2 + [pltpu.VMEM(tile, jnp.int32), dma((8,))]
+        out_shape=[wave] * 2 + [cell] * 4 + [pltpu.VMEM((2,) + tile[1:], F32),
+                                             pltpu.VMEM((2, tile[0], tile[2]), F32)],
+        in_specs=[hbm] * 12,
+        out_specs=[vmem] * 8,
+        scratch_shapes=[wave] * 5 + [cell] * 2 + [
+            pltpu.VMEM(tile, jnp.int32), lines, lines,
+            pltpu.SMEM((kinds,), F32), pltpu.SMEM((kinds,), F32), dma((12,))]
         + halos(pressure.shape) * 2 + halos(tile) * 3
-        + [cell, cell,
-           pltpu.VMEM((planes // 2 * rows, lateral), F32),
+        + [pltpu.VMEM((planes // 2 * rows, lateral), F32),
            pltpu.VMEM((blocks * slots, lateral // 2), F32),
            pltpu.VMEM((blocks * slots, lateral // 2), F32),
            pltpu.VMEM((blocks * slots, 128), F32),
            pltpu.VMEM((blocks * slots, 128), F32),
            dma((20,)), dma((20,)), dma((blocks,)), dma((blocks,)), dma((blocks,)), dma((blocks,))],
         compiler_params=pltpu.CompilerParams(
-            collective_id=0, has_side_effects=True, vmem_limit_bytes=40 * 1024 * 1024),
-    )(pressure, pressure_prev, courant, nonlinearity, absorption, own_map, slot_table,
+            collective_id=0, has_side_effects=True, vmem_limit_bytes=58 * 1024 * 1024),
+    )(pressure, pressure_prev, courant, nonlinearity, absorption, own_map.T, slot_table.T,
       displacement, displacement_prev, layer_labels, shear_table, viscosity_table)
+    return pl.pallas_call(
+        finish,
+        out_shape=waves + cells * 3,
+        in_specs=[vmem] * 8,
+        out_specs=[hbm] * 5,
+        scratch_shapes=[cell, dma((5,))],
+        compiler_params=pltpu.CompilerParams(vmem_limit_bytes=40 * 1024 * 1024),
+    )(*parts)
 
 
 def solution(mesh):

time: 49.8 us -> 31.1 us (0.62)
  local copies, waits for them, and re-layouts: 17.3 us -> 0 us
  Pallas kernels: 31.4 us -> 30.3 us
    unnamed x27 -> x0, local copies, waits for them, and re-layouts: 17.3 us -> none
    pallas_call x1 -> x2, Pallas kernels: 31.4 us -> 30.3 us  [the longest x1 27.8 us: local(): pl.pallas_call(functools.partial(kernel, capacity, slots), out_shape=[wav...]
where the time goes in v2:
time: 31.1 us; the launch traced here: 31 us
  Pallas kernels  30.3 us (97%)
  between operations  0.64 us (2%)
    pallas_call x1, Pallas kernels, local(): pl.pallas_call(functools.partial(kernel, capacity, slots), out_shape=[wav...  27.8 us
    pallas_call x1, Pallas kernels, local(): pl.pallas_call(finish, out_shape=waves + cells * 3, in_specs=[vmem] * 8,...  2.53 us

profile of v2, /device:TPU:0, one launch (start us, length us, event | category | flops | bytes accessed | tf_op | source)
XLA Modules:
  0.0 31.0 jit_solution(8627930961873646363)
XLA Ops:
  0.6 27.8 %shard_map.155 = (f32[24,16,768]{2,1,0:T(8,128)S(1)}, f32[24,16,768]{2,1,0:T(8,128)S(1)}, f32[16,32,384]{2,1,0:T(8,128)S(1)}, f32[16,32,384]{2,1,0:T(8,128)S(1)}...) custom-call(f32[24,16,768]{2,1,0:T(8,128)} %p_in.1, ...), custom_call_target="tpu_custom_call" | custom-call | tf_op jit(solution)/shard_map/pallas_call | solution.py:351
  28.4 2.5 %shard_map.156 = (f32[24,16,768]{2,1,0:T(8,128)}, f32[24,16,768]{2,1,0:T(8,128)}, f32[16,32,384]{2,1,0:T(8,128)}, f32[16,32,384]{2,1,0:T(8,128)}, f32[16,32,384]{2,1,0:T(8,128)}) custom-call(f32[24,16,768]{2,1,0:T(8,128)S(1)} %get-tuple-element.13.pm, f32[24,16,768]{2,1,0:T(8,128)S(1)} %get-tuple-element.14.pn, f32[16,32,384]{2,1,0:T(8,128)S(1)} %get-tuple-element.15.tf, ...), custom_call_target="tpu_custom_call" | custom-call | tf_op jit(solution)/shard_map/pallas_call | solution.py:371
